TPU v7x, 32 devices: a whole 2x2x4 slice. The times are simulated.
32 devices in a mesh: dp: 1, ep: 32 (over x, y, z, core).
Axes of the slice: x: 2, y: 2, z: 4, core: 2. Of those that a mesh axis runs over, the one named last changes fastest.
Arguments:
- x: bfloat16 [1, 32, 256, 1792], P('dp', 'ep')
- expert: int32 [1, 32, 256, 8], P('dp', 'ep')
- slot: int32 [1, 32, 256, 8], P('dp', 'ep')
- gate: float32 [1, 32, 256, 8], P('dp', 'ep')
- w_gate: bfloat16 [96, 1792, 2048], P('ep')
- w_up: bfloat16 [96, 1792, 2048], P('ep')
- w_down: bfloat16 [96, 2048, 1792], P('ep')
- s_gate: bfloat16 [1792, 2048], replicated
- s_up: bfloat16 [1792, 2048], replicated
- s_down: bfloat16 [2048, 1792], replicated
Outputs:
- y: bfloat16 [1, 32, 256, 1792], P('dp', 'ep')
All inputs are finite; a program needn't handle non-finite values.
Results may differ from a plain program's by a relative error of at most 0.009.
Values are sent between devices in bfloat16 or wider.
A program may use at most 2 GiB of HBM per device.

v0:
```python
import functools

import jax
import jax.numpy as jnp
from jax import lax
from jax.experimental import pallas as pl
from jax.experimental.pallas import tpu as pltpu
from jax.sharding import PartitionSpec as P

F32, BF16, I32 = jnp.float32, jnp.bfloat16, jnp.int32
MESH = pl.DeviceIdType.MESH

SLOTS = 26
PLANE = 8
LINE = 4
OWN = 3
BLOCKS = OWN * PLANE
PAD = 32
START = (0, 24, 48, 72)
ROWS = (24, 24, 24, 32)
BACK = ((0, 0, 24), (1, 0, 24), (2, 0, 24), (3, 0, 16), (3, 16, 16))
HALF = 16
COLS = 256
WIDE = 512
DEEP_F, DEEP_D = 3, 3
CALLS = 1 + LINE * OWN


def loop(n, body):
    lax.fori_loop(0, n, lambda i, c: (body(i), c)[1], 0)


def kernel(
    x, tab, w_gate, w_up, w_down, s_gate, s_up, s_down, y,
    lines, tabs, staged, slots, back, terms, shared, hidden, pick, pick_next, fbuf, dbuf,
    z_send, z_recv, d_send, d_recv, r_send, r_recv, p_send, p_recv, f_sem, d_sem,
):
    me = lax.axis_index("ep")
    mx, my, mz, mc = me // 16, (me // 8) % 2, (me // 2) % 4, me % 2
    place = (me // 8) * 2 + mc
    depth = x.shape[1]
    nf, nc = s_gate.shape[1] // WIDE, depth // COLS
    whole, tail = depth // WIDE, depth % WIDE
    nd = whole + (tail > 0)
    middle = (mz > 0) & (mz < 3)

    def peer(j):
        px, py, pc = (mx + j // 4) % 2, (my + (j // 2) % 2) % 2, (mc + j % 2) % 2
        return {"ep": ((px * 2 + py) * 4 + mz) * 2 + pc}, (px * 2 + py) * 2 + pc

    def line_peer(o):
        pz = (mz + 1 - 2 * (mz % 2), (mz + 2) % 4, 3 - mz)[o - 1]
        return {"ep": ((mx * 2 + my) * 4 + pz) * 2 + mc}

    def wide(ref, i):
        return ref.at[:, pl.ds(pl.multiple_of(i * WIDE, WIDE), WIDE)]

    def d_copy(ref, i, s):
        return pltpu.make_async_copy(wide(ref, i), dbuf.at[s], d_sem.at[s])

    def d_tail(ref, s):
        return pltpu.make_async_copy(ref.at[:, whole * WIDE :], dbuf.at[s, :, 0:tail], d_sem.at[s])

    def f_copies(gate, up, i, s):
        return [
            pltpu.make_async_copy(wide(gate, i), fbuf.at[s, 0], f_sem.at[s, 0]),
            pltpu.make_async_copy(wide(up, i), fbuf.at[s, 1], f_sem.at[s, 1]),
        ]

    def start_f(g):
        n, i, s = g // nf, g % nf, g % DEEP_F

        @pl.when(n == 0)
        def _():
            for c in f_copies(s_gate, s_up, i, s):
                c.start()

        @pl.when((n > 0) & (n < CALLS))
        def _():
            e = (n + OWN - 1) % OWN
            for c in f_copies(w_gate.at[e], w_up.at[e], i, s):
                c.start()

    def start_d(g):
        n, i, s = g // nd, g % nd, g % DEEP_D

        def start(ref):
            @pl.when(i < whole)
            def _():
                d_copy(ref, i, s).start()

            if tail:
                @pl.when(i == whole)
                def _():
                    d_tail(ref, s).start()

        @pl.when(n == 0)
        def _():
            start(s_down)

        @pl.when((n > 0) & (n < CALLS))
        def _():
            start(w_down.at[(n + OWN - 1) % OWN])

    loop(DEEP_F, start_f)
    loop(DEEP_D, start_d)

    barrier = pltpu.get_barrier_semaphore()
    for o in range(1, LINE):
        pl.semaphore_signal(barrier, inc=1, device_id=line_peer(o), device_id_type=MESH)
    for j in range(1, PLANE):
        pl.semaphore_signal(barrier, inc=1, device_id=peer(j)[0], device_id_type=MESH)
    def line_copies(q, src, to, slot):
        pairs = ((tab, x),) + tuple((tabs.at[o], lines.at[o]) for o in range(LINE - 1))
        return [
            pltpu.make_async_remote_copy(
                src_ref=ref, dst_ref=dst.at[slot - 1], send_sem=z_send.at[q, i], recv_sem=z_recv.at[slot - 1, i],
                device_id=line_peer(to), device_id_type=MESH,
            )
            for i, (ref, dst) in enumerate(zip(pairs[src], (tabs, lines)))
        ]

    LINE_SENDS = ((0, 1, 1), (0, 3, 3), (1, 3, 2), (3, 1, 2), (2, 1, 3))

    def line_start(q):
        for c in line_copies(q, *LINE_SENDS[q]):
            c.start()

    def line_wait(o):
        for c in line_copies(0, 0, o, o):
            c.wait_recv()

    def build(ref, height, o, start, rows, weigh):
        table = tab if o == 0 else tabs.at[o - 1]
        code = table[0:8, :].astype(I32) - mz * 1024
        gates = table[8:16, :]
        r = lax.broadcasted_iota(I32, (height, code.shape[1]), 0)
        v = r + (start - SLOTS * o)
        ok = (v >= 0) & (v < SLOTS) & (r < rows)

        def block(b):
            want = jnp.where(ok, v + b * SLOTS, -7)
            acc = jnp.zeros(want.shape, F32)
            for i in range(8):
                value = gates[i : i + 1, :] if weigh else jnp.float32(1)
                acc = jnp.where(want == code[i : i + 1, :], value, acc)
            ref[pl.ds(pl.multiple_of(b * height, height), height), :] = acc.astype(BF16)

        loop(BLOCKS, block)

    def tokens_of(o):
        return x if o == 0 else lines.at[o - 1]

    def slot_copy(k, j):
        device, there = peer(j)
        return pltpu.make_async_remote_copy(
            src_ref=staged.at[k, :, there, 0 : ROWS[k]], dst_ref=slots.at[k, :, place, 0 : ROWS[k]],
            send_sem=d_send.at[k, j], recv_sem=d_recv.at[k, j], device_id=device, device_id_type=MESH,
        )

    def stage(k):
        build(pick.at[0], PAD, k, START[k], ROWS[k], False)
        if k:
            build(pick.at[1], PAD, k - 1, START[k], ROWS[k], False)

        def columns(i):
            c = pl.ds(pl.multiple_of(i * COLS, COLS), COLS)
            out = jnp.dot(pick[0], tokens_of(k)[:, c], preferred_element_type=F32)
            if k:
                out += jnp.dot(pick[1], tokens_of(k - 1)[:, c], preferred_element_type=F32)
            staged[k, :, :, :, c] = out.astype(BF16).reshape(OWN, PLANE, PAD, COLS)

        loop(nc, columns)

    def dispatch(k):
        loop(PLANE - 1, lambda i: slot_copy(k, PLANE - 1 - i).start())
        slots[k, :, place] = staged[k, :, place]

    def ffn(n, read, write):
        def up(i):
            g = n * nf + i
            s = g % DEEP_F
            for c in f_copies(s_gate, s_up, 0, s):
                c.wait()
            z = read()
            a = jnp.dot(z, fbuf[s, 0], preferred_element_type=F32)
            b = jnp.dot(z, fbuf[s, 1], preferred_element_type=F32)
            hidden[:, pl.ds(pl.multiple_of(i * WIDE, WIDE), WIDE)] = (a * jax.nn.sigmoid(a) * b).astype(BF16)
            start_f(g + DEEP_F)

        def down(i):
            g = n * nd + i
            s = g % DEEP_D
            d_copy(s_down, 0, s).wait()
            write(
                pl.ds(pl.multiple_of(i * WIDE, WIDE), WIDE),
                jnp.dot(hidden[...], dbuf[s], preferred_element_type=F32),
            )
            start_d(g + DEEP_D)

        loop(nf, up)
        loop(whole, down)
        if tail:
            g = n * nd + whole
            s = g % DEEP_D
            d_tail(s_down, s).wait()
            write(
                pl.ds(whole * WIDE, tail),
                jnp.dot(hidden[...], dbuf[s, :, 0:tail], preferred_element_type=F32),
            )
            start_d(g + DEEP_D)

    def back_copy(p, j):
        k, r, rows = BACK[p]
        device, there = peer(j)
        return pltpu.make_async_remote_copy(
            src_ref=staged.at[k, :, there, r : r + rows], dst_ref=back.at[k, :, place, r : r + rows],
            send_sem=r_send.at[p, j], recv_sem=r_recv.at[p, j], device_id=device, device_id_type=MESH,
        )

    def send_back(p):
        loop(PLANE - 1, lambda i: back_copy(p, PLANE - 1 - i).start())
        k, r, rows = BACK[p]
        back[k, :, place, r : r + rows] = staged[k, :, place, r : r + rows]

    def term_copy(o, to, slot):
        return pltpu.make_async_remote_copy(
            src_ref=lines.at[o - 1], dst_ref=terms.at[slot], send_sem=p_send.at[o - 1], recv_sem=p_recv.at[slot],
            device_id=line_peer(to), device_id_type=MESH,
        )

    def term_wait(slot):
        term_copy(1, 1, slot).wait_recv()

    for k in range(LINE - 1):
        back[k, :, :, ROWS[k] : PAD] = jnp.zeros((OWN, PLANE, PAD - ROWS[k], depth), BF16)

    stage(0)
    pl.semaphore_wait(barrier, LINE - 1 + PLANE - 1)
    line_start(0)

    @pl.when(middle)
    def _():
        line_start(1)

    dispatch(0)

    def write_shared(c, value):
        shared[:, c] = value

    ffn(0, lambda: x[...], write_shared)
    line_wait(1)

    @pl.when(middle)
    def _():
        line_start(2)
        line_wait(3)
        line_start(3)

    stage(1)
    dispatch(1)

    def call(m):
        n = m + 1
        k, e = m // OWN, m % OWN
        for kk in range(LINE):
            @pl.when(m == kk * OWN)
            def _():
                def wait(i):
                    c = slot_copy(kk, i + 1)
                    c.wait_recv()
                    c.wait_send()

                loop(PLANE - 1, wait)

        def write(c, value):
            staged[k, e, :, :, c] = value.astype(BF16).reshape(PLANE, PAD, value.shape[1])

        ffn(n, lambda: slots[k, e].reshape(PLANE * PAD, depth), write)

        @pl.when(m == 1)
        def _():
            line_wait(2)

            @pl.when(middle)
            def _():
                line_start(4)

            stage(2)
            dispatch(2)

        @pl.when(m == 4)
        def _():
            @pl.when((mz == 0) | (mz == 3))
            def _():
                line_wait(3)

            stage(3)
            dispatch(3)

        @pl.when(m == 8)
        def _():
            send_back(2)

    loop(LINE * OWN, call)
    for p in (3, 4, 1, 0):
        send_back(p)

    def combine(o, pieces, write, wait=lambda: None):
        build(pick.at[0], PAD, o, START[o], ROWS[o], True)
        if o < LINE - 1:
            build(pick_next, HALF, o, START[o + 1], HALF, True)
        for p in pieces:
            loop(PLANE - 1, lambda i: back_copy(p, i + 1).wait_recv())
        wait()

        def columns(i):
            c = pl.ds(pl.multiple_of(i * COLS, COLS), COLS)

            def dot(weights, rows):
                return lax.dot_general(weights, rows, (((0,), (0,)), ((), ())), preferred_element_type=F32)

            out = dot(pick[0], back[o, :, :, :, c].reshape(BLOCKS * PAD, COLS))
            if o < LINE - 1:
                out += dot(pick_next[...], back[o + 1, :, :, 0:HALF, c].reshape(BLOCKS * HALF, COLS))
            write(c, out)

        loop(nc, columns)

    def pass_on(o, pieces, to, slot, add=None):
        def write(c, value):
            if add is not None:
                value += terms[add, :, c].astype(F32)
            lines[o - 1, :, c] = value.astype(BF16)

        combine(o, pieces, write, lambda: None if add is None else term_wait(add))
        term_copy(o, to, slot).start()

    for c in line_copies(0, *LINE_SENDS[0]):
        c.wait_send()

    @pl.when(middle)
    def _():
        for q in range(1, len(LINE_SENDS)):
            for c in line_copies(q, *LINE_SENDS[q]):
                c.wait_send()

    @pl.when((mz == 0) | (mz == 3))
    def _():
        pass_on(2, (2, 3), 1, 3)
        pass_on(3, (4,), 3, 2)

    @pl.when(middle)
    def _():
        pass_on(2, (2, 3), 2, 1)
        pass_on(3, (4,), 3, 2, 3)

    pass_on(1, (1,), 1, 0)

    @pl.when((mz == 0) | (mz == 3))
    def _():
        term_wait(1)

        def add(i):
            c = pl.ds(pl.multiple_of(i * COLS, COLS), COLS)
            shared[:, c] += terms[1, :, c].astype(F32)

        loop(nc, add)

    def stay(c, value):
        shared[:, c] += value

    combine(0, (0,), stay)
    term_wait(2)
    term_wait(0)

    def finish(i):
        c = pl.ds(pl.multiple_of(i * COLS, COLS), COLS)
        y[:, c] = (shared[:, c] + terms[0, :, c].astype(F32) + terms[2, :, c].astype(F32)).astype(BF16)

    loop(nc, finish)
    for o in range(1, LINE):
        term_copy(o, 1, 0).wait_send()
    for p in range(len(BACK)):
        loop(PLANE - 1, lambda i: back_copy(p, i + 1).wait_send())


def solution(mesh):
    def step(x, expert, slot, gate, w_gate, w_up, w_down, s_gate, s_up, s_down):
        tokens, depth = x.shape[2:]
        width = s_gate.shape[1]
        dev, e = expert[0, 0] // OWN, expert[0, 0] % OWN
        place = (dev // 8) * 2 + dev % 2
        code = ((dev // 2) % 4) * 1024 + (e * PLANE + place) * SLOTS + slot[0, 0]
        code = jnp.where(slot[0, 0] < SLOTS, code, -1)
        tab = jnp.concatenate([code.T.astype(F32), gate[0, 0].T], axis=0)
        vmem = pl.BlockSpec(memory_space=pltpu.VMEM)
        hbm = pl.BlockSpec(memory_space=pl.ANY)
        dma = pltpu.SemaphoreType.DMA
        rows = PLANE * PAD
        y = pl.pallas_call(
            kernel,
            name="moe",
            out_shape=jax.ShapeDtypeStruct((tokens, depth), BF16),
            in_specs=[vmem, vmem] + [hbm] * 6,
            out_specs=vmem,
            scratch_shapes=[
                pltpu.VMEM((LINE - 1, tokens, depth), BF16),
                pltpu.VMEM((LINE - 1, 16, tokens), F32),
                pltpu.VMEM((LINE, OWN, PLANE, PAD, depth), BF16),
                pltpu.VMEM((LINE, OWN, PLANE, PAD, depth), BF16),
                pltpu.VMEM((LINE, OWN, PLANE, PAD, depth), BF16),
                pltpu.VMEM((LINE, tokens, depth), BF16),
                pltpu.VMEM((tokens, depth), F32),
                pltpu.VMEM((rows, width), BF16),
                pltpu.VMEM((2, BLOCKS * PAD, tokens), BF16),
                pltpu.VMEM((BLOCKS * HALF, tokens), BF16),
                pltpu.VMEM((DEEP_F, 2, depth, WIDE), BF16),
                pltpu.VMEM((DEEP_D, width, WIDE), BF16),
                dma((5, 2)), dma((LINE - 1, 2)),
                dma((LINE, PLANE)), dma((LINE, PLANE)),
                dma((len(BACK), PLANE)), dma((len(BACK), PLANE)),
                dma((LINE - 1,)), dma((LINE,)),
                dma((DEEP_F, 2)), dma((DEEP_D,)),
            ],
            compiler_params=pltpu.CompilerParams(
                collective_id=0, has_side_effects=True, vmem_limit_bytes=67043328
            ),
        )(x[0, 0], tab, w_gate, w_up, w_down, s_gate, s_up, s_down)
        return y[None, None]

    row = P("dp", "ep", None, None)
    w = P("ep", None, None)
    s = P(None, None)
    return jax.shard_map(
        step, mesh=mesh, in_specs=(row, row, row, row, w, w, w, s, s, s), out_specs=row, check_vma=False
    )
```

profile of v0, /device:TPU:0, one launch (start us, length us, event | category | flops | bytes accessed | tf_op | source)
XLA Modules:
  0.0 222.1 jit_solution(338998068704388251)
XLA Ops:
  0.0 0.7 fusion.6
  0.8 1.3 pad_maximum_fusion.tab
  2.1 217.9 %moe.1 = bf16[256,1792]{1,0:T(8,128)(2,1)} custom-call(bf16[256,1792]{1,0:T(8,128)(2,1)} %bitcast.35, f32[16,256]{1,0:T(8,128)} %pad_maximum_fusion.tab, bf16[3,1792,2048]{2,1,0:T(8,128)(2,1)} %w_gate.1, bf16[3,1792,2048]{2,1,0:T(8,128)(2,1)} %w_up.1, bf16[3,2048,1792]{2,1,0:T(8,128)(2,1)} %w_down.1, bf16[1792,2048]{1,0:T(8,128)(2,1)} %s_gate.1, ...), custom_call_target="tpu_custom_call" | custom-call | tf_op jit(solution)/shard_map/moe/pallas_call | solution.py:401
  219.9 2.2 copy.12
where the time goes:
time: 222 us
  Pallas kernels  218 us (98%)
    pallas_call x1, Pallas kernels, step(): pl.pallas_call(kernel, name='moe', out_shape=jax.ShapeDtypeStruct((tokens...  218 us

commit v1 on v0

--- a/solution.py
+++ b/solution.py
@@ -158,16 +158,28 @@
             send_sem=d_send.at[k, j], recv_sem=d_recv.at[k, j], device_id=device, device_id_type=MESH,
         )
 
+    def early(k):
+        build(pick.at[1], PAD, k - 1, START[k], ROWS[k], False)
+
+        def columns(i):
+            c = pl.ds(pl.multiple_of(i * COLS, COLS), COLS)
+            out = jnp.dot(pick[1], tokens_of(k - 1)[:, c], preferred_element_type=F32)
+            staged[k, :, :, :, c] = out.astype(BF16).reshape(OWN, PLANE, PAD, COLS)
+
+        loop(nc, columns)
+
     def stage(k):
         build(pick.at[0], PAD, k, START[k], ROWS[k], False)
-        if k:
+        if k == LINE - 1:
             build(pick.at[1], PAD, k - 1, START[k], ROWS[k], False)
 
         def columns(i):
             c = pl.ds(pl.multiple_of(i * COLS, COLS), COLS)
             out = jnp.dot(pick[0], tokens_of(k)[:, c], preferred_element_type=F32)
-            if k:
+            if k == LINE - 1:
                 out += jnp.dot(pick[1], tokens_of(k - 1)[:, c], preferred_element_type=F32)
+            elif k:
+                out += staged[k, :, :, :, c].reshape(BLOCKS * PAD, COLS).astype(F32)
             staged[k, :, :, :, c] = out.astype(BF16).reshape(OWN, PLANE, PAD, COLS)
 
         loop(nc, columns)
@@ -249,6 +261,7 @@
         shared[:, c] = value
 
     ffn(0, lambda: x[...], write_shared)
+    early(1)
     line_wait(1)
 
     @pl.when(middle)
@@ -280,6 +293,7 @@
 
         @pl.when(m == 1)
         def _():
+            early(2)
             line_wait(2)
 
             @pl.when(middle)

time: 222 us -> 221 us (level)
  no operation moved by 1% of the time
where the time goes in v1:
time: 221 us
  Pallas kernels  216 us (98%)
    pallas_call x1, Pallas kernels, step(): pl.pallas_call(kernel, name='moe', out_shape=jax.ShapeDtypeStruct((tokens...  216 us

profile of v1, /device:TPU:0, one launch (start us, length us, event | category | flops | bytes accessed | tf_op | source)
XLA Modules:
  0.0 220.5 jit_solution(15299547165512191302)
XLA Ops:
  0.0 0.7 fusion.6
  0.8 1.3 pad_maximum_fusion.tab
  2.1 216.3 %moe.1 = bf16[256,1792]{1,0:T(8,128)(2,1)} custom-call(bf16[256,1792]{1,0:T(8,128)(2,1)} %bitcast.35, f32[16,256]{1,0:T(8,128)} %pad_maximum_fusion.tab, bf16[3,1792,2048]{2,1,0:T(8,128)(2,1)} %w_gate.1, bf16[3,1792,2048]{2,1,0:T(8,128)(2,1)} %w_up.1, bf16[3,2048,1792]{2,1,0:T(8,128)(2,1)} %w_down.1, bf16[1792,2048]{1,0:T(8,128)(2,1)} %s_gate.1, ...), custom_call_target="tpu_custom_call" | custom-call | tf_op jit(solution)/shard_map/moe/pallas_call | solution.py:415
  218.4 2.2 copy.12
